TPU v7x, 32 devices: a whole 2x2x4 slice. The times are simulated.
32 devices in a mesh: seq: 4 (over z), tensor: 2 (over x), dp: 4 (over y, core).
Axes of the slice: x: 2, y: 2, z: 4, core: 2. Of those that a mesh axis runs over, the one named last changes fastest.
Arguments:
- tokens: bfloat16 [4, 1024, 3072], P('dp', 'seq'), may hold values from -6 to 6
- cotangent: bfloat16 [4, 1024, 3072], P('dp', 'seq'), may hold values from -6 to 6
- qkv_weight: bfloat16 [3072, 3, 768], P(('seq', 'dp'), None, 'tensor'), may hold values from -0.109375 to 0.109375
- out_weight: bfloat16 [3072, 768], P(('seq', 'dp'), 'tensor'), may hold values from -0.21875 to 0.21875
Outputs:
- qkv_grad: float32 [3072, 3, 768], P(('seq', 'dp'), None, 'tensor')
- out_grad: float32 [3072, 768], P(('seq', 'dp'), 'tensor')
- branch_grad: bfloat16 [4, 1024, 3072], P('dp', 'seq', 'tensor')
All inputs are finite; a program needn't handle non-finite values.
Results may differ from a plain program's by a relative error of at most 0.025.
Values may be sent and summed in bfloat16 or wider, within the bound.
A program may use at most 128 MiB of HBM per device.

v0:
```python
import jax
import jax.numpy as jnp
from jax import lax
from jax.sharding import PartitionSpec as P

HD = 128
epsilon = 1e-06


def normalize(values):
    average = jnp.mean(values, axis=-1, keepdims=True)
    centered = values - average
    inverse = lax.rsqrt(jnp.mean(centered * centered, axis=-1, keepdims=True) + epsilon)
    return (centered * inverse, inverse)


def normalize_back(gradient, normed, inverse):
    mean_grad = jnp.mean(gradient, axis=-1, keepdims=True)
    mean_both = jnp.mean(gradient * normed, axis=-1, keepdims=True)
    return (gradient - mean_grad - normed * mean_both) * inverse


def local(tokens, cotangent, qkv_weight, out_weight):
    row_count = tokens.shape[1]
    feature_count = tokens.shape[2]
    column_count = out_weight.shape[1]
    head_count = column_count // HD
    score_scale = HD ** (-0.5)
    own_rows = qkv_weight.shape[0]
    grad_rows = cotangent[0]
    normed, inverse = normalize(tokens[0].astype(jnp.float32))
    unit_low = normed.astype(jnp.bfloat16)
    flat_weight = qkv_weight.reshape(own_rows, 3 * column_count)
    piece_qkv = lax.all_gather(flat_weight, ("seq", "dp"), axis=0, tiled=True)
    piece_out = lax.all_gather(out_weight, ("seq", "dp"), axis=0, tiled=True)
    piece_rows = piece_qkv.shape[0]
    left_rows = unit_low
    right_rows = grad_rows
    projected = jnp.dot(left_rows, piece_qkv, preferred_element_type=jnp.float32)
    attended_grad = jnp.dot(right_rows, piece_out, preferred_element_type=jnp.float32)
    full_qkv = piece_qkv
    projected, attended_grad, full_qkv = (projected, attended_grad, full_qkv)
    query_unit, query_inv = normalize(
        projected[:, :column_count].reshape(row_count, head_count, HD)
    )
    key_unit, key_inv = normalize(
        projected[:, column_count : 2 * column_count].reshape(row_count, head_count, HD)
    )
    query_low = query_unit.astype(jnp.bfloat16)
    key_value = jnp.stack(
        [
            key_unit.astype(jnp.bfloat16).reshape(row_count, column_count),
            projected[:, 2 * column_count :].astype(jnp.bfloat16),
        ]
    )
    grad_low = attended_grad.astype(jnp.bfloat16).reshape(row_count, head_count, HD)

    def scores_of(key_rows):
        piece_rows = key_rows.shape[0]
        return (
            jnp.einsum(
                "qhd,khd->hqk",
                query_low,
                key_rows.reshape(piece_rows, head_count, HD),
                preferred_element_type=jnp.float32,
            )
            * score_scale
        )

    every_pair = lax.all_gather(key_value, "seq", axis=1, tiled=True)
    piece_rows = every_pair.shape[1]
    exponent = jnp.exp(scores_of(every_pair[0]))
    add_exp_total = jnp.sum(exponent, axis=-1)
    weighted = jnp.einsum(
        "hqk,khd->qhd",
        exponent.astype(jnp.bfloat16),
        every_pair[1].reshape(piece_rows, head_count, HD),
        preferred_element_type=jnp.float32,
    )
    exp_total, weighted = (add_exp_total, weighted)
    attended_low = (weighted / exp_total.T[:, :, None]).astype(jnp.bfloat16)
    row_delta = jnp.sum(grad_low.astype(jnp.float32) * attended_low.astype(jnp.float32), axis=-1)
    piece_rows = every_pair.shape[1]
    key_rows = every_pair[0].reshape(piece_rows, head_count, HD)
    value_rows = every_pair[1].reshape(piece_rows, head_count, HD)
    probability = jnp.exp(scores_of(every_pair[0])) / exp_total[:, :, None]
    prob_grad = jnp.einsum("qhd,khd->hqk", grad_low, value_rows, preferred_element_type=jnp.float32)
    grad_score = (probability * (prob_grad - row_delta.T[:, :, None]) * score_scale).astype(
        jnp.bfloat16
    )
    query_part = jnp.einsum(
        "hqk,khd->qhd", grad_score, key_rows, preferred_element_type=jnp.float32
    )
    key_part = jnp.einsum("hqk,qhd->khd", grad_score, query_low, preferred_element_type=jnp.float32)
    value_part = jnp.einsum(
        "hqk,qhd->khd",
        probability.astype(jnp.bfloat16),
        grad_low,
        preferred_element_type=jnp.float32,
    )
    every_grad = jnp.stack(
        [key_part.reshape(piece_rows, column_count), value_part.reshape(piece_rows, column_count)]
    )
    pair_grad = lax.psum_scatter(
        every_grad.astype(jnp.bfloat16), "seq", scatter_dimension=1, tiled=True
    ).astype(jnp.float32)
    query_back = normalize_back(query_part, query_unit, query_inv)
    key_back = normalize_back(pair_grad[0].reshape(row_count, head_count, HD), key_unit, key_inv)
    qkv_low = jnp.concatenate(
        [
            query_back.reshape(row_count, column_count),
            key_back.reshape(row_count, column_count),
            pair_grad[1],
        ],
        axis=1,
    ).astype(jnp.bfloat16)
    inner_grad = jnp.einsum("rc,dc->rd", qkv_low, full_qkv, preferred_element_type=jnp.float32)
    attended_flat = attended_low.reshape(row_count, column_count)
    share_width = feature_count // lax.axis_size("tensor")
    whole_sum = lax.psum(inner_grad.astype(jnp.bfloat16), "tensor").astype(jnp.float32)
    branch = lax.dynamic_slice_in_dim(
        normalize_back(whole_sum, normed, inverse),
        lax.axis_index("tensor") * share_width,
        share_width,
        1,
    )
    left_rows = unit_low
    right_rows = grad_rows
    qkv_term = jnp.einsum(
        "rd,rc->dc", left_rows, qkv_low, preferred_element_type=jnp.float32
    ).reshape(lax.axis_size(("seq", "dp")) * own_rows, 3, column_count)
    out_term = jnp.einsum(
        "rd,rc->dc", right_rows, attended_flat, preferred_element_type=jnp.float32
    )
    summed = lax.psum_scatter(
        jnp.concatenate([qkv_term, out_term[:, None, :]], axis=1).astype(jnp.bfloat16),
        ("seq", "dp"),
        scatter_dimension=0,
        tiled=True,
    ).astype(jnp.float32)
    return (summed[:, :3], summed[:, 3], branch.astype(jnp.bfloat16)[None])


def solution(mesh):
    return jax.shard_map(
        local,
        mesh=mesh,
        in_specs=(
            P("dp", "seq", None),
            P("dp", "seq", None),
            P(("seq", "dp"), None, "tensor"),
            P(("seq", "dp"), "tensor"),
        ),
        out_specs=(
            P(("seq", "dp"), None, "tensor"),
            P(("seq", "dp"), "tensor"),
            P("dp", "seq", "tensor"),
        ),
        check_vma=False,
    )
```

profile of v0, /device:TPU:0, one launch (start us, length us, event | category | flops | bytes accessed | tf_op | source)
XLA Modules:
  0.0 413.4 jit_solution(1419548005790425770)
XLA Ops:
  7.2 2.0 copy.55
  10.0 1.7 convert_reduce_fusion
  12.3 67.3 %all-gather.4.cloned.1.call-done = bf16[3072,1152]{1,0:T(8,128)(2,1)} async-done(((bf16[192,1152]{1,0:T(8,128)(2,1)}), bf16[3072,1152]{1,0:T(8,128)(2,1)}) %all-gather.4.cloned.1.call-update) | async-done | bytes 7077904 | tf_op jit(solution)/shard_map/all_gather | solution.py:34
  79.6 5.3 %fusion.23 = f32[256,1152]{1,0:T(8,128)S(1)} fusion(bf16[3072,1152]{1,0:T(8,128)(2,1)} %all-gather.4.cloned.1.call-done, bf16[1,256,3072]{2,1,0:T(8,128)(2,1)S(1)} %copy-done.1, f32[256]{0:T(256)S(1)} %add_rsqrt_fusion.2, f32[256]{0:T(256)S(1)} %broadcast_multiply_fusion.8), kind=kOutput, calls=%fused_computation.35 | convolution fusion | flops 1815085056 | bytes 9832448 | tf_op jit(solution)/shard_map/dot_general | solution.py:39
  84.9 1.0 copy-done.7
  86.7 1.2 copy.27
  88.8 1.9 copy.29
  91.5 1.9 copy.28
  93.5 1.0 fusion.49
  94.5 2.2 fusion.59
  97.5 25.5 %all-gather.8.cloned.1.call-done = bf16[3072,384]{1,0:T(8,128)(2,1)} async-done(((bf16[192,384]{1,0:T(8,128)(2,1)}), bf16[3072,384]{1,0:T(8,128)(2,1)}) %all-gather.8.cloned.1.call-update) | async-done | bytes 2359312 | tf_op jit(solution)/shard_map/all_gather | solution.py:35
  123.0 2.6 fusion.39
  126.5 1.2 copy.31
  127.8 33.2 %all-gather.6.cloned.1.call-done = bf16[2,1024,384]{2,1,0:T(8,128)(2,1)} async-done(((bf16[2,256,384]{2,1,0:T(8,128)(2,1)}), bf16[2,1024,384]{2,1,0:T(8,128)(2,1)}) %all-gather.6.cloned.1.call-update) | async-done | bytes 1572880 | tf_op jit(solution)/shard_map/all_gather | solution.py:70
  161.0 2.7 fusion.58
  163.6 2.3 copy.30
  166.0 2.3 copy.35
  168.2 2.0 fusion.9
  170.3 1.7 fusion.27
  171.9 1.3 multiply_reduce_fusion.3
  173.3 1.1 multiply_convert_fusion
  174.4 1.2 copy-done.3
  175.6 1.3 convolution_convert_fusion.3
  176.9 2.3 copy.38
  179.2 2.3 copy.39
  181.5 2.7 pad_maximum_fusion.1
  184.5 2.3 fusion.57
  187.6 1.7 copy.44
  189.3 29.4 %reduce-scatter.3.cloned.1.call-done = bf16[2,256,384]{2,1,0:T(8,128)(2,1)} async-done(((bf16[2,1024,384]{2,1,0:T(8,128)(2,1)}), bf16[2,256,384]{2,1,0:T(8,128)(2,1)}) %reduce-scatter.3.cloned.1.call-update) | async-done | bytes 393232 | tf_op jit(solution)/shard_map/reduce_scatter | solution.py:104
  218.7 1.9 slice_convert_fusion.1
  220.6 1.9 copy.40
  222.5 1.2 multiply_reduce_fusion.1
  224.5 1.9 copy.42
  227.2 1.9 copy.41
  229.1 1.6 fusion.46
  231.4 6.5 %convolution_convert_fusion.2 = bf16[256,3072]{1,0:T(8,128)(2,1)} fusion(bf16[3072,1152]{1,0:T(8,128)(2,1)} %all-gather.4.cloned.1.call-done, bf16[256,384]{1,0:T(8,128)(2,1)S(1)} %copy-done.13, bf16[256,384]{1,0:T(8,128)(2,1)S(1)} %fusion.46, bf16[256,384]{1,0:T(8,128)(2,1)S(1)} %copy-done.10), kind=kOutput, calls=%fused_computation.7 | convolution fusion | flops 1814495232 | bytes 9240576 | tf_op jit(solution)/shard_map/rc,dc->rd/dot_general | solution.py:117
  238.0 3.5 fusion
  241.5 0.9 fusion.48
  242.4 2.2 copy.45
  244.5 5.5 %convolution_convert_fusion = bf16[3072,3,384]{2,0,1:T(8,128)(2,1)} fusion(bf16[3,384,256]{2,1,0:T(8,128)(2,1)} %bitcast.107, bf16[1,256,3072]{2,1,0:T(8,128)(2,1)S(1)} %copy-done.1, f32[256]{0:T(256)S(1)} %copy-done.17, f32[256]{0:T(256)S(1)} %copy-done.19), kind=kOutput, calls=%fused_computation.1 | convolution fusion | flops 1818624000 | bytes 9242624 | tf_op jit(solution)/shard_map/rd,rc->dc/dot_general | solution.py:129
  250.1 8.4 %pad_maximum_fusion = bf16[3072,4,384]{2,0,1:T(8,128)(2,1)} fusion(bf16[3072,1,384]{2,0,1:T(8,128)(2,1)} %fusion, bf16[3072,3,384]{2,0,1:T(8,128)(2,1)} %convolution_convert_fusion), kind=kLoop, calls=%fused_computation | loop fusion | flops 4718592 | bytes 18874368 | tf_op jit(solution)/shard_map/concatenate | solution.py:136
  258.5 29.9 %all-reduce.2.cloned.1.call-done = bf16[256,3072]{1,0:T(8,128)(2,1)} async-done(((bf16[256,3072]{1,0:T(8,128)(2,1)}), bf16[256,3072]{1,0:T(8,128)(2,1)}) %all-reduce.2.cloned.1.call-update) | async-done | bytes 1572880 | tf_op jit(solution)/shard_map/psum | solution.py:120
  288.4 1.9 convert_element_type.80
  290.3 1.1 convert_reduce_fusion.1
  291.4 1.2 fusion.43
  292.6 111.0 %reduce-scatter.5.cloned.1.call-done = bf16[192,4,384]{2,0,1:T(8,128)(2,1)} async-done(((bf16[3072,4,384]{2,0,1:T(8,128)(2,1)}), bf16[192,4,384]{2,0,1:T(8,128)(2,1)}) %reduce-scatter.5.cloned.1.call-update) | async-done | bytes 589840 | tf_op jit(solution)/shard_map/reduce_scatter | solution.py:135
  403.6 1.2 convert_element_type.78
  405.6 1.0 slice.52
  (74 shorter events, 9.7 us)
Async XLA Ops:
  7.2 115.9 %copy-start = (bf16[1,256,3072]{2,1,0:T(8,128)(2,1)S(1)}, bf16[1,256,3072]{2,1,0:T(8,128)(2,1)}, u32[]{:S(2)}) copy-start(bf16[1,256,3072]{2,1,0:T(8,128)(2,1)} %param.5) | copy-start | bytes 4718596
  7.2 4.6 %copy-start.1 = (bf16[1,256,3072]{2,1,0:T(8,128)(2,1)S(1)}, bf16[1,256,3072]{2,1,0:T(8,128)(2,1)}, u32[]{:S(2)}) copy-start(bf16[1,256,3072]{2,1,0:T(8,128)(2,1)} %param.4) | copy-start | bytes 4718596
  7.2 72.5 %all-gather.4.cloned.1.call-start = ((), (), s32[]{:S(2)}) async-start(), calls=%async_computation.2 | async-start | bytes 7520256 | tf_op jit(solution)/shard_map/all_gather | solution.py:34
  9.2 113.8 %all-gather.8.cloned.1.call-start = ((), (), s32[]{:S(2)}) async-start(), calls=%async_computation.4 | async-start | bytes 2506752 | tf_op jit(solution)/shard_map/all_gather | solution.py:35
  10.0 151.0 %all-gather.6.cloned.1.call-start = ((), (), s32[]{:S(2)}) async-start(), calls=%async_computation.3 | async-start | bytes 1966080 | tf_op jit(solution)/shard_map/all_gather | solution.py:70
  11.7 73.2 %copy-start.18 = (f32[256]{0:T(256)}, f32[256]{0:T(256)S(1)}, u32[]{:S(2)}) copy-start(f32[256]{0:T(256)S(1)} %broadcast_multiply_fusion.8) | copy-start | bytes 3076
  12.3 72.6 %copy-start.16 = (f32[256]{0:T(256)}, f32[256]{0:T(256)S(1)}, u32[]{:S(2)}) copy-start(f32[256]{0:T(256)S(1)} %add_rsqrt_fusion.2) | copy-start | bytes 3076
  84.9 1.0 copy-start.7
  87.9 8.8 %copy-start.2 = (f32[256,384]{0,1:T(8,128)}, f32[256,384]{0,1:T(8,128)S(1)}, u32[]{:S(2)}) copy-start(f32[256,384]{0,1:T(8,128)S(1)} %copy.27) | copy-start | bytes 1179652
  97.5 121.2 %reduce-scatter.3.cloned.1.call-start = ((), (), s32[]{:S(2)}) async-start(), calls=%async_computation.5 | async-start | bytes 1966080 | tf_op jit(solution)/shard_map/reduce_scatter | solution.py:104
  168.2 2.0 copy-start.15
  170.2 1.7 copy-start.12
  174.4 1.2 copy-start.3
  184.2 104.2 %all-reduce.2.cloned.1.call-start = ((), (), s32[]{:S(2)}) async-start(), calls=%async_computation.7 | async-start | bytes 3145728 | tf_op jit(solution)/shard_map/psum | solution.py:120
  189.3 39.8 %copy-start.6 = (f32[256,384]{1,0:T(8,128)S(1)}, f32[256,384]{1,0:T(8,128)}, u32[]{:S(2)}) copy-start(f32[256,384]{1,0:T(8,128)} %copy.29) | copy-start | bytes 1179652
  229.1 2.3 copy-start.10
  229.1 2.3 copy-start.13
  230.7 0.7 copy-start.8
  237.9 3.6 copy-start.9
  237.9 3.6 copy-start.11
  237.9 165.7 %reduce-scatter.5.cloned.1.call-start = ((), (), s32[]{:S(2)}) async-start(), calls=%async_computation.6 | async-start | bytes 10027008 | tf_op jit(solution)/shard_map/reduce_scatter | solution.py:135
  238.0 3.6 copy-start.14
  238.0 6.6 %copy-start.17 = (f32[256]{0:T(256)S(1)}, f32[256]{0:T(256)}, u32[]{:S(2)}) copy-start(f32[256]{0:T(256)} %copy-done.16) | copy-start | bytes 3076
  238.0 6.6 %copy-start.19 = (f32[256]{0:T(256)S(1)}, f32[256]{0:T(256)}, u32[]{:S(2)}) copy-start(f32[256]{0:T(256)} %copy-done.18) | copy-start | bytes 3076
  288.4 1.9 copy-start.4
  403.6 2.0 copy-start.5
Sparse Core Ops, SparseCore 0:
  10.9 68.7 all-gather.3
  81.9 41.0 all-gather.7
  125.2 35.7 all-gather.5
  184.4 34.2 reduce-scatter.2
  238.0 50.3 all-reduce.1
  292.4 111.2 reduce-scatter.4
where the time goes:
time: 415 us; the launch traced here: 413 us
  waiting for transfers between devices  297 us (72%)
  local copies, waits for them, and re-layouts  40.1 us (10%)
  matrix products  33.2 us (8%)
  other arithmetic  28.3 us (7%)
  between operations  14.4 us (3%)
    reduce_scatter x1, waiting for transfers between devices, local(): lax.psum_scatter(jnp.concatenate([qkv_term, out_term[:, None, :]], axis=1...  111 us
    all_gather x1, waiting for transfers between devices, local(): piece_qkv = lax.all_gather(flat_weight, ('seq', 'dp'), axis=0, tiled=True)  67.3 us
    all_gather x1, waiting for transfers between devices, local(): every_pair = lax.all_gather(key_value, 'seq', axis=1, tiled=True)  33.2 us
    psum x1, waiting for transfers between devices, local(): lax.psum(inner_grad.astype(jnp.bfloat16), 'tensor').astype(jnp.float32)  29.9 us
    reduce_scatter x1, waiting for transfers between devices, local(): lax.psum_scatter(every_grad.astype(jnp.bfloat16), 'seq', scatter_dimensio...  29.4 us
    all_gather x1, waiting for transfers between devices, local(): piece_out = lax.all_gather(out_weight, ('seq', 'dp'), axis=0, tiled=True)  25.5 us
    concatenate x1, other arithmetic, local(): jnp.concatenate([qkv_term, out_term[:, None, :]], axis=1)  8.4 us
  transfers between devices with their start and end apart: 6, of which 6 were waited for; matrix products, arithmetic and copies ran while one was open for 13% of the time, Pallas kernels for 0%

commit v1 on v0

--- a/solution.py
+++ b/solution.py
@@ -31,8 +31,13 @@
     normed, inverse = normalize(tokens[0].astype(jnp.float32))
     unit_low = normed.astype(jnp.bfloat16)
     flat_weight = qkv_weight.reshape(own_rows, 3 * column_count)
-    piece_qkv = lax.all_gather(flat_weight, ("seq", "dp"), axis=0, tiled=True)
-    piece_out = lax.all_gather(out_weight, ("seq", "dp"), axis=0, tiled=True)
+    piece_qkv, piece_out = jnp.split(
+        lax.all_gather(
+            jnp.concatenate([flat_weight, out_weight], axis=1), ("seq", "dp"), axis=0, tiled=True
+        ),
+        [flat_weight.shape[1]],
+        axis=1,
+    )
     piece_rows = piece_qkv.shape[0]
     left_rows = unit_low
     right_rows = grad_rows

time: 415 us -> 401 us (0.966)
  waiting for transfers between devices: 297 us -> 285 us
    all_gather x2 -> x1, waiting for transfers between devices: 92.8 us -> 83.3 us  [local(): lax.all_gather(jnp.concatenate([flat_weight, out_weight], axis=1), ('seq'...]
  transfers between devices with their start and end apart: 6 -> 5, of which waited for: 6 -> 5; matrix products, arithmetic and copies ran while one was open for 13% -> 9% of each run, Pallas kernels for 0% -> 0%
where the time goes in v1:
time: 401 us; the launch traced here: 400 us
  waiting for transfers between devices  285 us (71%)
  local copies, waits for them, and re-layouts  37.4 us (9%)
  matrix products  33.7 us (8%)
  other arithmetic  29.6 us (7%)
  between operations  14.1 us (4%)
    reduce_scatter x1, waiting for transfers between devices, local(): lax.psum_scatter(jnp.concatenate([qkv_term, out_term[:, None, :]], axis=1...  111 us
    all_gather x1, waiting for transfers between devices, local(): lax.all_gather(jnp.concatenate([flat_weight, out_weight], axis=1), ('seq'...  83.3 us
    all_gather x1, waiting for transfers between devices, local(): every_pair = lax.all_gather(key_value, 'seq', axis=1, tiled=True)  31.1 us
    psum x1, waiting for transfers between devices, local(): lax.psum(inner_grad.astype(jnp.bfloat16), 'tensor').astype(jnp.float32)  29.9 us
    reduce_scatter x1, waiting for transfers between devices, local(): lax.psum_scatter(every_grad.astype(jnp.bfloat16), 'seq', scatter_dimensio...  29.4 us
    concatenate x1, other arithmetic, local(): jnp.concatenate([qkv_term, out_term[:, None, :]], axis=1)  8.4 us
  transfers between devices with their start and end apart: 5, of which 5 were waited for; matrix products, arithmetic and copies ran while one was open for 9% of the time, Pallas kernels for 0%

profile of v1, /device:TPU:0, one launch (start us, length us, event | category | flops | bytes accessed | tf_op | source)
XLA Modules:
  0.0 399.9 jit_solution(17067136962596566154)
XLA Ops:
  7.2 1.2 copy.52
  8.4 1.8 pad_maximum_fusion.2
  11.2 83.3 %all-gather.3.cloned.1.call-done = bf16[3072,1536]{1,0:T(8,128)(2,1)} async-done(((bf16[192,1536]{1,0:T(8,128)(2,1)}), bf16[3072,1536]{1,0:T(8,128)(2,1)}) %all-gather.3.cloned.1.call-update) | async-done | bytes 9437200 | tf_op jit(solution)/shard_map/all_gather | solution.py:35
  94.5 5.3 %fusion.2 = f32[256,1152]{1,0:T(8,128)S(1)} fusion(bf16[3072,1536]{1,0:T(8,128)(2,1)} %all-gather.3.cloned.1.call-done, bf16[1,256,3072]{2,1,0:T(8,128)(2,1)S(1)} %copy-done.1, f32[256]{0:T(256)S(1)} %add_rsqrt_fusion.2, f32[256]{0:T(256)S(1)} %broadcast_multiply_fusion.8), kind=kOutput, calls=%fused_computation.3 | convolution fusion | flops 1815085056 | bytes 9832448 | tf_op jit(solution)/shard_map/dot_general | solution.py:44
  101.7 1.2 copy.25
  103.0 0.8 mul.130
  103.8 1.9 copy.27
  106.5 1.9 copy.26
  108.4 2.2 fusion.68
  110.6 1.7 pad_maximum_fusion.4
  112.4 1.2 copy.29
  113.7 3.2 fusion.46
  116.8 31.1 %all-gather.5.cloned.1.call-done = bf16[2,1024,384]{2,1,0:T(8,128)(2,1)} async-done(((bf16[2,256,384]{2,1,0:T(8,128)(2,1)}), bf16[2,1024,384]{2,1,0:T(8,128)(2,1)}) %all-gather.5.cloned.1.call-update) | async-done | bytes 1572880 | tf_op jit(solution)/shard_map/all_gather | solution.py:75
  147.9 2.7 fusion.67
  150.6 2.3 copy.28
  152.9 2.3 copy.32
  155.2 2.0 fusion.16
  157.2 1.7 fusion.34
  158.9 1.3 multiply_reduce_fusion.3
  160.2 1.1 multiply_convert_fusion
  161.4 1.1 copy-done.3
  162.5 1.3 convolution_convert_fusion.2
  163.8 2.3 copy.35
  166.1 2.3 copy.36
  168.3 2.7 pad_maximum_fusion.1
  171.3 2.3 fusion.66
  174.4 1.7 copy.41
  176.2 29.4 %reduce-scatter.3.cloned.1.call-done = bf16[2,256,384]{2,1,0:T(8,128)(2,1)} async-done(((bf16[2,1024,384]{2,1,0:T(8,128)(2,1)}), bf16[2,256,384]{2,1,0:T(8,128)(2,1)}) %reduce-scatter.3.cloned.1.call-update) | async-done | bytes 393232 | tf_op jit(solution)/shard_map/reduce_scatter | solution.py:109
  205.6 1.9 slice_convert_fusion.1
  207.4 1.9 copy.37
  209.3 1.2 multiply_reduce_fusion.1
  210.6 0.8 mul.146
  211.3 1.9 copy.39
  214.0 1.9 copy.38
  215.9 1.6 fusion.55
  218.2 6.5 %fusion.5 = bf16[256,3072]{1,0:T(8,128)(2,1)} fusion(bf16[3072,1536]{1,0:T(8,128)(2,1)} %all-gather.3.cloned.1.call-done, bf16[256,384]{1,0:T(8,128)(2,1)S(1)} %copy-done.13, bf16[256,384]{1,0:T(8,128)(2,1)S(1)} %fusion.55, bf16[256,384]{1,0:T(8,128)(2,1)S(1)} %copy-done.10), kind=kOutput, calls=%fused_computation.11 | convolution fusion | flops 1814495232 | bytes 9240576 | tf_op jit(solution)/shard_map/rc,dc->rd/dot_general | solution.py:122
  224.8 3.5 fusion.4
  228.3 0.9 fusion.57
  229.2 2.1 copy.42
  231.4 5.5 %convolution_convert_fusion = bf16[3072,3,384]{2,0,1:T(8,128)(2,1)} fusion(bf16[3,384,256]{2,1,0:T(8,128)(2,1)} %bitcast.106, bf16[1,256,3072]{2,1,0:T(8,128)(2,1)S(1)} %copy-done.1, f32[256]{0:T(256)S(1)} %copy-done.16, f32[256]{0:T(256)S(1)} %copy-done.18), kind=kOutput, calls=%fused_computation.5 | convolution fusion | flops 1818624000 | bytes 9242624 | tf_op jit(solution)/shard_map/rd,rc->dc/dot_general | solution.py:134
  236.9 8.4 %pad_maximum_fusion = bf16[3072,4,384]{2,0,1:T(8,128)(2,1)} fusion(bf16[3072,1,384]{2,0,1:T(8,128)(2,1)} %fusion.4, bf16[3072,3,384]{2,0,1:T(8,128)(2,1)} %convolution_convert_fusion), kind=kLoop, calls=%fused_computation | loop fusion | flops 4718592 | bytes 18874368 | tf_op jit(solution)/shard_map/concatenate | solution.py:141
  245.3 29.9 %all-reduce.2.cloned.1.call-done = bf16[256,3072]{1,0:T(8,128)(2,1)} async-done(((bf16[256,3072]{1,0:T(8,128)(2,1)}), bf16[256,3072]{1,0:T(8,128)(2,1)}) %all-reduce.2.cloned.1.call-update) | async-done | bytes 1572880 | tf_op jit(solution)/shard_map/psum | solution.py:125
  275.2 1.9 convert_element_type.84
  277.1 1.1 convert_reduce_fusion.1
  278.2 1.2 fusion.52
  279.4 111.0 %reduce-scatter.5.cloned.1.call-done = bf16[192,4,384]{2,0,1:T(8,128)(2,1)} async-done(((bf16[3072,4,384]{2,0,1:T(8,128)(2,1)}), bf16[192,4,384]{2,0,1:T(8,128)(2,1)}) %reduce-scatter.5.cloned.1.call-update) | async-done | bytes 589840 | tf_op jit(solution)/shard_map/reduce_scatter | solution.py:140
  390.4 1.2 convert_element_type.82
  392.4 1.0 slice.52
  (71 shorter events, 7.3 us)
Async XLA Ops:
  7.2 106.5 %copy-start = (bf16[1,256,3072]{2,1,0:T(8,128)(2,1)S(1)}, bf16[1,256,3072]{2,1,0:T(8,128)(2,1)}, u32[]{:S(2)}) copy-start(bf16[1,256,3072]{2,1,0:T(8,128)(2,1)} %param.5) | copy-start | bytes 4718596
  7.2 3.1 copy-start.1
  7.2 87.3 %all-gather.3.cloned.1.call-start = ((), (), s32[]{:S(2)}) async-start(), calls=%async_computation.2 | async-start | bytes 10027008 | tf_op jit(solution)/shard_map/all_gather | solution.py:35
  10.2 137.7 %all-gather.5.cloned.1.call-start = ((), (), s32[]{:S(2)}) async-start(), calls=%async_computation.3 | async-start | bytes 1966080 | tf_op jit(solution)/shard_map/all_gather | solution.py:75
  10.6 89.2 %copy-start.17 = (f32[256]{0:T(256)}, f32[256]{0:T(256)S(1)}, u32[]{:S(2)}) copy-start(f32[256]{0:T(256)S(1)} %broadcast_multiply_fusion.8) | copy-start | bytes 3076
  11.2 88.6 %copy-start.15 = (f32[256]{0:T(256)}, f32[256]{0:T(256)S(1)}, u32[]{:S(2)}) copy-start(f32[256]{0:T(256)S(1)} %add_rsqrt_fusion.2) | copy-start | bytes 3076
  99.8 1.1 copy-start.7
  102.9 7.7 %copy-start.2 = (f32[256,384]{0,1:T(8,128)}, f32[256,384]{0,1:T(8,128)S(1)}, u32[]{:S(2)}) copy-start(f32[256,384]{0,1:T(8,128)S(1)} %copy.25) | copy-start | bytes 1179652
  112.3 93.2 %reduce-scatter.3.cloned.1.call-start = ((), (), s32[]{:S(2)}) async-start(), calls=%async_computation.4 | async-start | bytes 1966080 | tf_op jit(solution)/shard_map/reduce_scatter | solution.py:109
  155.2 2.0 copy-start.19
  157.2 1.7 copy-start.12
  161.3 1.1 copy-start.3
  171.1 104.1 %all-reduce.2.cloned.1.call-start = ((), (), s32[]{:S(2)}) async-start(), calls=%async_computation.6 | async-start | bytes 3145728 | tf_op jit(solution)/shard_map/psum | solution.py:125
  176.2 39.7 %copy-start.6 = (f32[256,384]{1,0:T(8,128)S(1)}, f32[256,384]{1,0:T(8,128)}, u32[]{:S(2)}) copy-start(f32[256,384]{1,0:T(8,128)} %copy.27) | copy-start | bytes 1179652
  215.9 2.3 copy-start.10
  215.9 2.3 copy-start.13
  217.5 0.7 copy-start.8
  224.7 3.6 copy-start.9
  224.7 3.6 copy-start.11
  224.7 165.7 %reduce-scatter.5.cloned.1.call-start = ((), (), s32[]{:S(2)}) async-start(), calls=%async_computation.5 | async-start | bytes 10027008 | tf_op jit(solution)/shard_map/reduce_scatter | solution.py:140
  224.8 3.6 copy-start.14
  224.8 6.6 %copy-start.16 = (f32[256]{0:T(256)S(1)}, f32[256]{0:T(256)}, u32[]{:S(2)}) copy-start(f32[256]{0:T(256)} %copy-done.15) | copy-start | bytes 3076
  224.8 6.6 %copy-start.18 = (f32[256]{0:T(256)S(1)}, f32[256]{0:T(256)}, u32[]{:S(2)}) copy-start(f32[256]{0:T(256)} %copy-done.17) | copy-start | bytes 3076
  275.2 1.9 copy-start.4
  390.4 2.0 copy-start.5
Sparse Core Ops, SparseCore 0:
  10.9 83.6 all-gather.2
  112.4 35.4 all-gather.4
  171.2 34.2 reduce-scatter.2
  224.8 50.3 all-reduce.1
  279.2 111.2 reduce-scatter.4
